TPU v7x, 256 devices: a 4x2x16 block of a 4x16x16 slice. The times are simulated.
256 devices in a mesh: rep: 2 (over y), step: 32 (over z, core), patch: 4 (over x).
Axes of the slice: x: 4, y: 2, z: 16, core: 2. Of those that a mesh axis runs over, the one named last changes fastest.
The devices are a block of a 4x16x16 slice.
Arguments:
- latent_old: float32 [64, 1024, 64], P(('rep', 'step'), 'patch'), parts along dimension 0, may hold values from -6 to 6
- noise_start: float32 [2048, 64], P(('rep', 'patch')), parts along dimension 0, may hold values from -6 to 6
- step_index: int32 [64], P(('rep', 'step')), parts along dimension 0, may hold values from 0 to 998
- sigma_table: float32 [1000], replicated, may hold values from 0.02 to 1
- mod_weight: bfloat16 [256, 9216], replicated, may hold values from -0.375 to 0.375
- embed_weight: bfloat16 [64, 3072], replicated, may hold values from -0.75 to 0.75
- embed_bias: float32 [3072], replicated, may hold values from -3 to 3
- query_weight: bfloat16 [3072, 1536], P('step'), may hold values from -0.109375 to 0.109375
- query_gain: float32 [128], replicated, may hold values from 0.1 to 1.9
- stale_keys: bfloat16 [64, 1280, 1536], P(('rep', 'step'), 'patch'), parts along dimension 0, may hold values from -640 to 640
- stale_values: bfloat16 [64, 1280, 1536], P(('rep', 'step'), 'patch'), parts along dimension 0, may hold values from -6 to 6
- out_weight: bfloat16 [3072, 1536], P('step'), may hold values from -0.3125 to 0.3125
- final_weight: bfloat16 [3072, 64], replicated, may hold values from -0.109375 to 0.109375
Outputs:
- latent_new: float32 [64, 1024, 64], P(('rep', 'step'), 'patch'), parts along dimension 0
There are 2 independent parts, one for each index of `rep`. A program takes and returns all parts, laid end to end along the dimension named above; an argument that names none is the same for every part. Nothing has to cross between parts.
All inputs are finite; a program needn't handle non-finite values.
Results may differ from a plain program's by a relative error of at most 0.012.
The roundings to bfloat16 on the way count: a program that leaves them out, or rounds other values in their place, can miss the bound.
Values may be sent and summed in bfloat16 or wider, within the bound.
No kernel may reach another device: no remote copies, remote signals or barrier semaphores. Data moves between devices by JAX's collectives and lax.ppermute only.
A program may use at most 128 MiB of HBM per device.

v0:
```python
import math
import jax
import jax.numpy as jnp
from jax import lax
from jax.sharding import Mesh
from jax.sharding import PartitionSpec as P

D = 3072
HEAD = 128
FREQ = 256
STEP = ("step_0", "step_1")
REP_STEP = ("rep", "step_0", "step_1")
epsilon = 1e-06


def from_everyone(shard, axis):
    copies = jnp.broadcast_to(shard, (lax.axis_size(axis), *shard.shape))
    return lax.all_to_all(copies, axis, split_axis=0, concat_axis=0, tiled=True)


def in_order(pieces, dim):
    dims = list(pieces.shape[1:])
    dims[dim] *= pieces.shape[0]
    return jnp.moveaxis(pieces, 0, dim).reshape(dims)


def gather_directly(shard, axis, dim):
    pieces = from_everyone(shard, axis)
    return in_order(pieces, dim)


def side_by_side(arrays, axis, dim, along):
    ends, at = ([], 0)
    for a in arrays[:-1]:
        at += a.shape[along]
        ends.append(at)
    both = jnp.concatenate(arrays, axis=along)
    return tuple(jnp.split(gather_directly(both, axis, dim), ends, axis=along))


def neutral_like(shard, identity):
    return jnp.zeros_like(shard) + jnp.asarray(identity, shard.dtype)


def entering(shard, axes, combine, identity):
    before = start = neutral_like(shard, identity)
    running = shard
    for axis in reversed(axes):
        devices, here = (lax.axis_size(axis), lax.axis_index(axis))
        pieces = lax.all_gather(running.astype(jnp.bfloat16), axis)
        inside, running = (start, start)
        for k in range(devices):
            passed = k < here
            running = combine(running, pieces[k].astype(shard.dtype))
            inside = jnp.where(passed, running, inside)
        before = combine(inside, before)
    return before


def layer_norm(values_in):
    row_mean = jnp.mean(values_in, axis=-1, keepdims=True)
    centered = values_in - row_mean
    row_var = jnp.mean(centered * centered, axis=-1, keepdims=True)
    return centered * lax.rsqrt(row_var + epsilon)


def time_embed(sigma_now):
    half_count = FREQ // 2
    frequency = jnp.exp(
        -math.log(10000.0) * jnp.arange(half_count).astype(jnp.float32) / half_count
    )
    angles = 1000.0 * sigma_now * frequency
    return jnp.concatenate([jnp.cos(angles), jnp.sin(angles)])


def project_back(attended, weight_rows):
    return lax.dot_general(
        attended, weight_rows, (((1,), (1,)), ((), ())), preferred_element_type=jnp.float32
    )


def norm_queries(raw_queries, query_gain):
    token_count = raw_queries.shape[0]
    head_count = raw_queries.shape[1] // HEAD
    queries = raw_queries.reshape(token_count, head_count, HEAD)
    queries = (
        queries
        * lax.rsqrt(jnp.mean(queries * queries, axis=-1, keepdims=True) + epsilon)
        * query_gain
    )
    return queries.astype(jnp.bfloat16)


def empty_state(queries):
    token_count = queries.shape[0]
    head_count = queries.shape[1]
    return (
        jnp.full((head_count, token_count), -jnp.inf, jnp.float32),
        jnp.zeros((head_count, token_count), jnp.float32),
        jnp.zeros((head_count, token_count, HEAD), jnp.float32),
    )


def attend_block(queries, state_tuple, key_piece, value_piece):
    head_count = queries.shape[1]
    row_count = key_piece.shape[0]
    key_split = key_piece.reshape(row_count, head_count, HEAD)
    value_split = value_piece.reshape(row_count, head_count, HEAD)
    run_peak, run_total, run_sum = state_tuple
    scores = jnp.einsum(
        "qhd,khd->hqk", queries, key_split, preferred_element_type=jnp.float32
    ) / math.sqrt(HEAD)
    new_peak = jnp.max(scores, axis=-1)
    rescale = jnp.exp(run_peak - new_peak)
    exp_weights = jnp.exp(scores - new_peak[..., None])
    run_total = run_total * rescale + jnp.sum(exp_weights, axis=-1)
    run_sum = run_sum * rescale[..., None] + jnp.einsum(
        "hqk,khd->hqd",
        exp_weights.astype(jnp.bfloat16),
        value_split,
        preferred_element_type=jnp.float32,
    )
    return (new_peak, run_total, run_sum)


def finish_heads(state_tuple):
    final_peak, final_total, final_sum = state_tuple
    blended = final_sum / final_total[..., None]
    token_count = blended.shape[1]
    return jnp.transpose(blended, (1, 0, 2)).reshape(token_count, -1).astype(jnp.bfloat16)


def per_device(
    latent_old,
    noise_start,
    step_index,
    sigma_table,
    mod_weight,
    embed_weight,
    embed_bias,
    query_weight,
    query_gain,
    stale_keys,
    stale_values,
    out_weight,
    final_weight,
):
    step_slot = step_index[0]
    table_slots = jnp.arange(sigma_table.shape[0])
    sigma_now = jnp.sum(jnp.where(table_slots == step_slot, sigma_table, 0.0))
    sigma_next = jnp.sum(jnp.where(table_slots == step_slot + 1, sigma_table, 0.0))
    embedded = jax.nn.silu(time_embed(sigma_now)).astype(jnp.bfloat16)
    modulate = jnp.dot(embedded[None, :], mod_weight, preferred_element_type=jnp.float32)[0]
    width = D
    shift_vec = modulate[:width]
    scale_vec = modulate[width : 2 * width]
    gate_vec = modulate[2 * width :]
    latent = latent_old[0]
    token_count = latent.shape[0]
    hidden = (
        jnp.dot(latent.astype(jnp.bfloat16), embed_weight, preferred_element_type=jnp.float32)
        + embed_bias
    )
    normed = (layer_norm(hidden) * (1.0 + scale_vec) + shift_vec).astype(jnp.bfloat16)
    raw_queries = jnp.dot(
        normed,
        lax.all_gather(query_weight, STEP, axis=0, tiled=True),
        preferred_element_type=jnp.float32,
    )
    queries = norm_queries(raw_queries, query_gain)
    pieces = side_by_side((stale_keys[0], stale_values[0]), "patch", 0, 1)
    final_state = attend_block(queries, empty_state(queries), pieces[0], pieces[1])
    attended = finish_heads(final_state)
    branch = project_back(attended, lax.all_gather(out_weight, STEP, axis=0, tiled=True))
    mixed = hidden + gate_vec * branch
    velocity = jnp.dot(
        layer_norm(mixed).astype(jnp.bfloat16), final_weight, preferred_element_type=jnp.float32
    )
    drift_term = velocity * (sigma_next - sigma_now)
    flat_term = drift_term.reshape(-1, 128)

    def add_terms(earlier, later):
        return earlier + later

    prefix = entering(flat_term, STEP, add_terms, jnp.zeros_like(flat_term))
    result = noise_start + (prefix + flat_term).reshape(token_count, -1)
    return result[None]


def solution(mesh):
    torus = Mesh(
        mesh.devices.reshape(mesh.shape["rep"], 16, 2, mesh.shape["patch"]),
        ("rep", "step_0", "step_1", "patch"),
    )
    placed = (
        P(REP_STEP, "patch", None),
        P(("rep", "patch"), None),
        P(REP_STEP),
        P(),
        P(),
        P(),
        P(),
        P(STEP, None),
        P(),
        P(REP_STEP, "patch", None),
        P(REP_STEP, "patch", None),
        P(STEP, None),
        P(),
    )
    return jax.shard_map(
        per_device,
        mesh=torus,
        in_specs=placed,
        out_specs=P(REP_STEP, "patch", None),
        check_vma=False,
    )
```

profile of v0, /device:TPU:36, one launch (start us, length us, event | category | flops | bytes accessed | tf_op | source)
XLA Modules:
  0.0 225.6 jit_solution(14928748804721785456)
XLA Ops:
  6.6 0.7 all-gather.3.cloned.1.call-update
  7.4 0.7 all-gather.5.cloned.1.call-update
  8.1 1.7 pad_maximum_fusion
  9.8 4.1 %broadcast_in_dim.17 = bf16[4,320,3072]{2,1,0:T(8,128)(2,1)} broadcast(bf16[320,3072]{1,0:T(8,128)(2,1)S(1)} %pad_maximum_fusion), dimensions={1,2} | broadcast | bytes 9830400 | tf_op jit(solution)/shard_map/broadcast_in_dim | solution.py:17
  13.9 24.9 %all-to-all-start = ((bf16[4,320,3072]{2,1,0:T(8,128)(2,1)}), bf16[4,320,3072]{2,1,0:T(8,128)(2,1)}, u32[]{:S(2)}, u32[]{:S(2)}) async-start(bf16[4,320,3072]{2,1,0:T(8,128)(2,1)} %broadcast_in_dim.17), calls=%async_computation | async-start | bytes 15728640 | tf_op jit(solution)/shard_map/all_to_all | solution.py:18
  39.4 0.6 select_reduce_fusion
  42.0 1.5 fusion.46
  43.5 0.5 multiply_reduce_fusion.2
  44.0 3.2 %fusion.49 = f32[1,9216]{1,0:T(1,128)S(1)} fusion(bf16[256,1]{0,1:T(2,128)(2,1)S(1)} %reshape.197, bf16[256,9216]{1,0:T(8,128)(2,1)} %param.17), kind=kOutput, calls=%fused_computation.92 | convolution fusion | flops 4718592 | bytes 4755968 | tf_op jit(solution)/shard_map/dot_general | solution.py:153
  47.2 58.1 %all-to-all-done = bf16[4,320,3072]{2,1,0:T(8,128)(2,1)} async-done(((bf16[4,320,3072]{2,1,0:T(8,128)(2,1)}), bf16[4,320,3072]{2,1,0:T(8,128)(2,1)}, u32[]{:S(2)}, u32[]{:S(2)}) %all-to-all-start) | async-done | bytes 7864352 | tf_op jit(solution)/shard_map/all_to_all | solution.py:18
  105.3 5.5 %fusion.44 = (bf16[1280,1536]{1,0:T(8,128)(2,1)}, bf16[1280,1536]{1,0:T(8,128)(2,1)}) fusion(bf16[1280,3072]{1,0:T(8,128)(2,1)} %bitcast.6), kind=kLoop, calls=%fused_computation.87 | loop fusion | bytes 15728640 | tf_op jit(solution)/shard_map/split | solution.py:38
  110.9 6.3 %copy.31 = bf16[1280,1536]{0,1:T(8,128)(2,1)} copy(bf16[1280,1536]{1,0:T(8,128)(2,1)} %get-tuple-element.8) | data formatting | bytes 7864320 | tf_op jit(solution)/shard_map/split | solution.py:38
  117.2 6.2 %copy.28 = bf16[1280,1536]{0,1:T(8,128)(2,1)} copy(bf16[1280,1536]{1,0:T(8,128)(2,1)} %get-tuple-element.7) | data formatting | bytes 7864320 | tf_op jit(solution)/shard_map/split | solution.py:38
  123.4 6.9 %fusion.7 = f32[256,1536]{0,1:T(8,128)S(1)} fusion(bf16[3072,1536]{1,0:T(8,128)(2,1)} %all-gather.3.cloned.1.call-done, f32[256,3072]{1,0:T(8,128)S(1)} %get-tuple-element.15, f32[3072]{0:T(1024)S(1)} %get-tuple-element.12, f32[3072]{0:T(1024)S(1)} %get-tuple-element.13, f32[256]{0:T(256)S(1)} %add_rsqrt_fusion.2, f32[256]{0:T(256)S(1)} %broadcast_multiply_fusion.1), kind=kOutput, calls=%fused_computation.15 | convolution fusion | flops 2419851264 | bytes 14182400 | tf_op jit(solution)/shard_map/dot_general | solution.py:165
  130.3 0.1 multiply_reduce_fusion.3
  130.5 2.4 %multiply_reduce_fusion = (f32[12,256]{1,0:T(8,128)S(1)}, f32[12,256,1280]{2,1,0:T(8,128)S(1)}) fusion(bf16[1280,12,128]{0,2,1:T(8,128)(2,1)S(1)} %bitcast.39, f32[256,12,128]{0,2,1:T(8,128)S(1)} %bitcast.41, f32[128]{0:T(128)S(1)} %copy-done.8, f32[256,12]{0,1:T(8,128)S(1)} %add_rsqrt_fusion), kind=kOutput, calls=%fused_computation.1 | convolution fusion | flops 1015673856 | bytes 21258752 | tf_op jit(solution)/shard_map/qhd,khd->hqk/dot_general | solution.py:110
  132.9 3.3 %fusion = f32[12,256]{1,0:T(8,128)S(1)} fusion(f32[12,256,1280]{2,1,0:T(8,128)S(1)} %get-tuple-element.17, f32[12,256]{1,0:T(8,128)S(1)} %get-tuple-element.16), kind=kLoop, calls=%fused_computation.2 | loop fusion | flops 11793408 | bytes 15753216 | tf_op jit(solution)/shard_map/reduce_sum | solution.py:116
  136.3 2.2 copy-done.2
  138.5 11.0 %fusion.10 = bf16[256,12,128]{0,2,1:T(8,128)(2,1)} fusion(bf16[1280,12,128]{0,2,1:T(8,128)(2,1)} %bitcast.42, f32[12,256,1280]{2,1,0:T(8,128)} %copy-done.2, f32[12,256]{1,0:T(8,128)S(1)} %get-tuple-element.16, f32[256,12]{0,1:T(8,128)S(1)} %bitcast_add_fusion.1, f32[256,12]{0,1:T(8,128)S(1)} %multiply_bitcast_fusion), kind=kOutput, calls=%fused_computation.19 | convolution fusion | flops 1019609088 | bytes 20484096 | tf_op jit(solution)/shard_map/hqk,khd->hqd/dot_general | solution.py:117
  149.5 27.1 %all-gather.5.cloned.1.call-done = bf16[3072,1536]{1,0:T(8,128)(2,1)} async-done(((bf16[96,1536]{1,0:T(8,128)(2,1)}), bf16[3072,1536]{1,0:T(8,128)(2,1)}) %all-gather.5.cloned.1.call-update) | async-done | bytes 9437200 | tf_op jit(solution)/shard_map/all_gather | solution.py:174
  176.6 5.6 %fusion.47 = (f32[256]{0:T(256)S(1)}, f32[256,3072]{1,0:T(8,128)S(1)}) fusion(f32[256,3072]{1,0:T(8,128)S(1)} %get-tuple-element.15, bf16[256,1536]{0,1:T(8,128)(2,1)} %bitcast.46, bf16[3072,1536]{1,0:T(8,128)(2,1)} %all-gather.5.cloned.1.call-done, f32[3072]{0:T(1024)S(1)} %get-tuple-element.11), kind=kOutput, calls=%fused_computation.90 | convolution fusion | flops 2418278144 | bytes 16528384 | tf_op jit(solution)/shard_map/dot_general | solution.py:77
  182.3 0.5 multiply_reduce_fusion.1
  182.7 0.5 copy-done.4
  183.2 0.7 fusion.48
  183.9 0.1 copy.32
  184.0 0.1 convert_element_type.175
  184.1 1.9 all_gather.16
  186.1 31.1 %all_gather.17 = bf16[16,128,128]{2,1,0:T(8,128)(2,1)S(1)} all-gather(bf16[1,128,128]{2,1,0:T(8,128)(2,1)S(1)} %get-tuple-element.9), channel_id=1, replica_groups=mesh['rep'=2,'step_0'=16,'step_1'=2,'patch'=4] {'step_0'}, dimensions={0}, use_global_device_ids=true | all-gather | bytes 557056 | tf_op jit(solution)/shard_map/all_gather | solution.py:50
  217.3 0.1 select_n.183
  217.4 0.1 reshape.194
  217.6 0.1 fusion.36
  218.1 0.7 add_bitcast_fusion
  (39 shorter events, 0.8 us)
Async XLA Ops:
  6.5 35.4 %copy-start = (bf16[64,3072]{1,0:T(8,128)(2,1)S(1)}, bf16[64,3072]{1,0:T(8,128)(2,1)}, u32[]{:S(2)}) copy-start(bf16[64,3072]{1,0:T(8,128)(2,1)} %param.18) | copy-start | bytes 1179652
  6.6 116.8 %all-gather.3.cloned.1.call-start = ((), (), s32[]{:S(2)}) async-start(), calls=%async_computation.1 | async-start | bytes 9732096 | tf_op jit(solution)/shard_map/all_gather | solution.py:167
  7.3 169.3 %all-gather.5.cloned.1.call-start = ((), (), s32[]{:S(2)}) async-start(), calls=%async_computation.2 | async-start | bytes 9732096 | tf_op jit(solution)/shard_map/all_gather | solution.py:174
  13.9 25.5 %copy-start.7 = (f32[1000]{0:T(1024)S(1)}, f32[1000]{0:T(1024)}, u32[]{:S(2)}) copy-start(f32[1000]{0:T(1024)} %param.16) | copy-start | bytes 12004
  13.9 28.1 %copy-start.6 = (f32[3072]{0:T(1024)S(1)}, f32[3072]{0:T(1024)}, u32[]{:S(2)}) copy-start(f32[3072]{0:T(1024)} %param.19) | copy-start | bytes 36868
  13.9 91.4 %all-to-all-start = ((bf16[4,320,3072]{2,1,0:T(8,128)(2,1)}), bf16[4,320,3072]{2,1,0:T(8,128)(2,1)}, u32[]{:S(2)}, u32[]{:S(2)}) async-start(bf16[4,320,3072]{2,1,0:T(8,128)(2,1)} %broadcast_in_dim.17), calls=%async_computation | async-start | bytes 15728640 | tf_op jit(solution)/shard_map/all_to_all | solution.py:18
  123.4 7.1 %copy-start.3 = (bf16[1280,1536]{0,1:T(8,128)(2,1)S(1)}, bf16[1280,1536]{0,1:T(8,128)(2,1)}, u32[]{:S(2)}) copy-start(bf16[1280,1536]{0,1:T(8,128)(2,1)} %copy.28) | copy-start | bytes 11796484
  123.4 7.1 %copy-start.8 = (f32[128]{0:T(128)S(1)}, f32[128]{0:T(128)}, u32[]{:S(2)}) copy-start(f32[128]{0:T(128)} %param.21) | copy-start | bytes 1540
  132.9 5.5 %copy-start.2 = (f32[12,256,1280]{2,1,0:T(8,128)}, f32[12,256,1280]{2,1,0:T(8,128)S(1)}, u32[]{:S(2)}) copy-start(f32[12,256,1280]{2,1,0:T(8,128)S(1)} %get-tuple-element.17) | copy-start | bytes 47185924
  182.2 1.0 copy-start.4
  182.7 36.0 %copy-start.1 = (bf16[64,3072]{1,0:T(8,128)(2,1)S(1)}, bf16[64,3072]{1,0:T(8,128)(2,1)}, u32[]{:S(2)}) copy-start(bf16[64,3072]{1,0:T(8,128)(2,1)} %param.18) | copy-start | bytes 1179652
  183.2 34.8 %copy-start.5 = (f32[256,64]{0,1:T(8,128)S(1)}, f32[256,64]{0,1:T(8,128)}, u32[]{:S(2)}) copy-start(f32[256,64]{0,1:T(8,128)} %param.14) | copy-start | bytes 196612
Sparse Core Ops, SparseCore 0:
  9.2 91.4 all-gather.2
  102.6 73.9 all-gather.4
where the time goes:
time: 226 us
  waiting for transfers between devices  86.8 us (38%)
  blocking collectives  33 us (15%)
  matrix products  31.3 us (14%)
  local copies, waits for them, and re-layouts  25.8 us (11%)
  starting transfers between devices  24.9 us (11%)
  between operations  16.2 us (7%)
  other arithmetic  7.65 us (3%)
    all_to_all x1, waiting for transfers between devices, from_everyone(): return lax.all_to_all(copies, axis, split_axis=0, concat_axis=0, tiled=True)  58.1 us
    all_gather x2, blocking collectives, entering(): pieces = lax.all_gather(running.astype(jnp.bfloat16), axis)  33 us
    all_gather x1, waiting for transfers between devices, per_device(): lax.all_gather(out_weight, STEP, axis=0, tiled=True)  27.1 us
    all_to_all x1, starting transfers between devices, from_everyone(): return lax.all_to_all(copies, axis, split_axis=0, concat_axis=0, tiled=True)  24.9 us
    split x3, local copies, waits for them, and re-layouts, side_by_side(): return tuple(jnp.split(gather_directly(both, axis, dim), ends, axis=along))  18.1 us
    dot_general x1, matrix products, attend_block(): jnp.einsum('hqk,khd->hqd', exp_weights.astype(jnp.bfloat16), value_split,...  11 us
    dot_general x1, matrix products, per_device(): jnp.dot(normed, lax.all_gather(query_weight, STEP, axis=0, tiled=True), p...  6.91 us
    dot_general x1, matrix products, project_back(): lax.dot_general(attended, weight_rows, (((1,), (1,)), ((), ())), preferre...  5.63 us
  transfers between devices with their start and end apart: 3, of which 2 were waited for; matrix products, arithmetic and copies ran while one was open for 24% of the time, Pallas kernels for 0%

commit v1 on v0

--- a/solution.py
+++ b/solution.py
@@ -145,6 +145,12 @@
     out_weight,
     final_weight,
 ):
+
+    def wait_ends(z_in, mesh_ax):
+        return jnp.concatenate(
+            lax.all_to_all(jnp.stack(lax.axis_size(mesh_ax) * [z_in]), mesh_ax, 0, 0), axis=0
+        )
+
     step_slot = step_index[0]
     table_slots = jnp.arange(sigma_table.shape[0])
     sigma_now = jnp.sum(jnp.where(table_slots == step_slot, sigma_table, 0.0))
@@ -171,7 +177,7 @@
     pieces = side_by_side((stale_keys[0], stale_values[0]), "patch", 0, 1)
     final_state = attend_block(queries, empty_state(queries), pieces[0], pieces[1])
     attended = finish_heads(final_state)
-    branch = project_back(attended, lax.all_gather(out_weight, STEP, axis=0, tiled=True))
+    branch = project_back(attended, wait_ends(out_weight, STEP))
     mixed = hidden + gate_vec * branch
     velocity = jnp.dot(
         layer_norm(mixed).astype(jnp.bfloat16), final_weight, preferred_element_type=jnp.float32

time: 226 us -> 642 us (2.84)
  waiting for transfers between devices: 86.8 us -> 399 us
  blocking collectives: 33 us -> 134 us
    all_gather x1, waiting for transfers between devices: 0.01 us -> 274 us  [per_device(): lax.all_gather(query_weight, STEP, axis=0, tiled=True)]
    all_to_all x0 -> x1, blocking collectives: none -> 90.3 us  [from_everyone(): return lax.all_to_all(copies, axis, split_axis=0, concat_axis=0, tiled=True)]
    all_to_all x1, waiting for transfers between devices: 58.1 us -> 124 us  [wait_ends(): lax.all_to_all(jnp.stack(lax.axis_size(mesh_ax) * [z_in]), mesh_ax, 0, 0)]
    all_gather x1 -> x0, waiting for transfers between devices: 27.1 us -> none  [per_device(): lax.all_gather(out_weight, STEP, axis=0, tiled=True)]
    all_gather x2, blocking collectives: 33 us -> 43.6 us  [entering(): pieces = lax.all_gather(running.astype(jnp.bfloat16), axis)]
  transfers between devices with their start and end apart: 3 -> 2, of which waited for: 2 -> 2; matrix products, arithmetic and copies ran while one was open for 24% -> 7% of each run, Pallas kernels for 0% -> 0%
where the time goes in v1:
time: 642 us; the launch traced here: 639 us
  waiting for transfers between devices  399 us (62%)
  blocking collectives  134 us (21%)
  matrix products  31 us (5%)
  local copies, waits for them, and re-layouts  25.9 us (4%)
  starting transfers between devices  25 us (4%)
  between operations  16.4 us (3%)
  other arithmetic  7.74 us (1%)
    all_gather x1, waiting for transfers between devices, per_device(): lax.all_gather(query_weight, STEP, axis=0, tiled=True)  274 us
    all_to_all x1, waiting for transfers between devices, wait_ends(): lax.all_to_all(jnp.stack(lax.axis_size(mesh_ax) * [z_in]), mesh_ax, 0, 0)  124 us
    all_to_all x1, blocking collectives, from_everyone(): return lax.all_to_all(copies, axis, split_axis=0, concat_axis=0, tiled=True)  90.3 us
    all_gather x2, blocking collectives, entering(): pieces = lax.all_gather(running.astype(jnp.bfloat16), axis)  43.6 us
    all_to_all x1, starting transfers between devices, wait_ends(): lax.all_to_all(jnp.stack(lax.axis_size(mesh_ax) * [z_in]), mesh_ax, 0, 0)  24.9 us
    split x3, local copies, waits for them, and re-layouts, side_by_side(): return tuple(jnp.split(gather_directly(both, axis, dim), ends, axis=along))  15.8 us
  transfers between devices with their start and end apart: 2, of which 2 were waited for; matrix products, arithmetic and copies ran while one was open for 7% of the time, Pallas kernels for 0%

profile of v1, /device:TPU:36, one launch (start us, length us, event | category | flops | bytes accessed | tf_op | source)
XLA Modules:
  0.0 639.2 jit_solution(2129132933471285612)
XLA Ops:
  6.6 1.7 pad_maximum_fusion
  8.3 1.0 broadcast_in_dim.17
  9.3 90.3 %all_to_all.10 = bf16[4,320,3072]{2,1,0:T(8,128)(2,1)} all-to-all(bf16[4,320,3072]{2,1,0:T(8,128)(2,1)S(1)} %broadcast_in_dim.17), channel_id=1, replica_groups=mesh['rep'=2,'step_0'=16,'step_1'=2,'patch'=4] {'patch'}, dimensions={0} | all-to-all | bytes 15728640 | tf_op jit(solution)/shard_map/all_to_all | solution.py:18
  99.6 4.6 stack.2
  104.3 24.9 %all-to-all-start.1 = ((bf16[32,96,1536]{2,1,0:T(8,128)(2,1)}), bf16[32,96,1536]{2,1,0:T(8,128)(2,1)}, u32[]{:S(2)}, u32[]{:S(2)}) async-start(bf16[32,96,1536]{2,1,0:T(8,128)(2,1)} %stack.2), calls=%async_computation.1 | async-start | bytes 18874368 | tf_op jit(solution)/shard_map/all_to_all | solution.py:151
  129.2 0.7 all-gather.2.cloned.1.call-update
  130.6 0.7 select_reduce_fusion
  133.4 1.5 fusion.46
  135.0 0.5 multiply_reduce_fusion.2
  135.4 3.3 fusion.49
  138.7 0.9 copy-done.3
  139.6 3.6 fusion.44
  143.2 6.1 copy.31
  149.3 6.2 copy.28
  155.5 274.1 %all-gather.2.cloned.1.call-done = bf16[3072,1536]{1,0:T(8,128)(2,1)} async-done(((bf16[96,1536]{1,0:T(8,128)(2,1)}), bf16[3072,1536]{1,0:T(8,128)(2,1)}) %all-gather.2.cloned.1.call-update) | async-done | bytes 9437200 | tf_op jit(solution)/shard_map/all_gather | solution.py:173
  429.6 6.8 %fusion.7 = f32[256,1536]{0,1:T(8,128)S(1)} fusion(bf16[3072,1536]{1,0:T(8,128)(2,1)} %all-gather.2.cloned.1.call-done, f32[256,3072]{1,0:T(8,128)S(1)} %get-tuple-element.15, f32[3072]{0:T(1024)S(1)} %get-tuple-element.12, f32[3072]{0:T(1024)S(1)} %get-tuple-element.13, f32[256]{0:T(256)S(1)} %add_rsqrt_fusion.2, f32[256]{0:T(256)S(1)} %broadcast_multiply_fusion.1), kind=kOutput, calls=%fused_computation.15 | convolution fusion | flops 2419851264 | bytes 14182400 | tf_op jit(solution)/shard_map/dot_general | solution.py:171
  436.4 0.1 multiply_reduce_fusion.3
  436.6 2.4 multiply_reduce_fusion
  439.0 3.3 fusion
  442.3 2.2 copy-done.2
  444.5 10.7 %fusion.10 = bf16[256,12,128]{0,2,1:T(8,128)(2,1)} fusion(bf16[1280,12,128]{0,2,1:T(8,128)(2,1)} %bitcast.44, f32[12,256,1280]{2,1,0:T(8,128)} %copy-done.2, f32[12,256]{1,0:T(8,128)S(1)} %get-tuple-element.16, f32[256,12]{0,1:T(8,128)S(1)} %bitcast_add_fusion.1, f32[256,12]{0,1:T(8,128)S(1)} %multiply_bitcast_fusion), kind=kOutput, calls=%fused_computation.19 | convolution fusion | flops 1019609088 | bytes 20484096 | tf_op jit(solution)/shard_map/hqk,khd->hqd/dot_general | solution.py:117
  455.2 124.4 %all-to-all-done.1 = bf16[32,96,1536]{2,1,0:T(8,128)(2,1)} async-done(((bf16[32,96,1536]{2,1,0:T(8,128)(2,1)}), bf16[32,96,1536]{2,1,0:T(8,128)(2,1)}, u32[]{:S(2)}, u32[]{:S(2)}) %all-to-all-start.1) | async-done | bytes 9437216 | tf_op jit(solution)/shard_map/all_to_all | solution.py:151
  579.6 5.6 fusion.47
  585.3 0.5 multiply_reduce_fusion.1
  585.8 0.5 copy-done.5
  586.3 0.7 fusion.48
  586.9 0.1 copy.32
  587.1 0.1 convert_element_type.175
  587.2 1.9 all_gather.12
  589.1 41.7 %all_gather.13 = bf16[16,128,128]{2,1,0:T(8,128)(2,1)S(1)} all-gather(bf16[1,128,128]{2,1,0:T(8,128)(2,1)S(1)} %get-tuple-element.9), channel_id=1, replica_groups=mesh['rep'=2,'step_0'=16,'step_1'=2,'patch'=4] {'step_0'}, dimensions={0}, use_global_device_ids=true | all-gather | bytes 557056 | tf_op jit(solution)/shard_map/all_gather | solution.py:50
  631.3 0.1 fusion.36
  631.7 0.7 add_bitcast_fusion
  (42 shorter events, 1.0 us)
Async XLA Ops:
  6.5 126.9 %copy-start = (bf16[64,3072]{1,0:T(8,128)(2,1)S(1)}, bf16[64,3072]{1,0:T(8,128)(2,1)}, u32[]{:S(2)}) copy-start(bf16[64,3072]{1,0:T(8,128)(2,1)} %param.18) | copy-start | bytes 1179652
  9.3 90.3 %copy-start.6 = (bf16[96,1536]{1,0:T(8,128)(2,1)S(1)}, bf16[96,1536]{1,0:T(8,128)(2,1)}, u32[]{:S(2)}) copy-start(bf16[96,1536]{1,0:T(8,128)(2,1)} %param.24) | copy-start | bytes 884740
  104.3 26.4 %copy-start.9 = (f32[1000]{0:T(1024)S(1)}, f32[1000]{0:T(1024)}, u32[]{:S(2)}) copy-start(f32[1000]{0:T(1024)} %param.16) | copy-start | bytes 12004
  104.3 29.2 %copy-start.8 = (f32[3072]{0:T(1024)S(1)}, f32[3072]{0:T(1024)}, u32[]{:S(2)}) copy-start(f32[3072]{0:T(1024)} %param.19) | copy-start | bytes 36868
  104.3 475.4 %all-to-all-start.1 = ((bf16[32,96,1536]{2,1,0:T(8,128)(2,1)}), bf16[32,96,1536]{2,1,0:T(8,128)(2,1)}, u32[]{:S(2)}, u32[]{:S(2)}) async-start(bf16[32,96,1536]{2,1,0:T(8,128)(2,1)} %stack.2), calls=%async_computation.1 | async-start | bytes 18874368 | tf_op jit(solution)/shard_map/all_to_all | solution.py:151
  129.2 300.4 %all-gather.2.cloned.1.call-start = ((), (), s32[]{:S(2)}) async-start(), calls=%async_computation.2 | async-start | bytes 9732096 | tf_op jit(solution)/shard_map/all_gather | solution.py:173
  134.9 4.7 copy-start.3
  429.6 7.0 %copy-start.4 = (bf16[1280,1536]{0,1:T(8,128)(2,1)S(1)}, bf16[1280,1536]{0,1:T(8,128)(2,1)}, u32[]{:S(2)}) copy-start(bf16[1280,1536]{0,1:T(8,128)(2,1)} %copy.28) | copy-start | bytes 11796484
  429.6 7.0 %copy-start.10 = (f32[128]{0:T(128)S(1)}, f32[128]{0:T(128)}, u32[]{:S(2)}) copy-start(f32[128]{0:T(128)} %param.21) | copy-start | bytes 1540
  439.0 5.5 copy-start.2
  585.3 1.0 copy-start.5
  585.7 46.6 %copy-start.1 = (bf16[64,3072]{1,0:T(8,128)(2,1)S(1)}, bf16[64,3072]{1,0:T(8,128)(2,1)}, u32[]{:S(2)}) copy-start(bf16[64,3072]{1,0:T(8,128)(2,1)} %param.18) | copy-start | bytes 1179652
  586.3 45.5 %copy-start.7 = (f32[256,64]{0,1:T(8,128)S(1)}, f32[256,64]{0,1:T(8,128)}, u32[]{:S(2)}) copy-start(f32[256,64]{0,1:T(8,128)} %param.14) | copy-start | bytes 196612
Sparse Core Ops, SparseCore 0:
  131.8 297.6 all-gather.1
